TPU v7x, 8 devices: a whole 2x2x1 slice. The times are simulated.
8 devices in a mesh: dp: 1 (over z), sp: 2 (over y), cp: 4 (over x, core).
Axes of the slice: x: 2, y: 2, z: 1, core: 2. Of those that a mesh axis runs over, the one named last changes fastest.
Arguments:
- x_act: bfloat16 [32, 96, 14, 1024], P('dp', 'sp', None, 'cp')
- w_one: bfloat16 [3, 3, 1024, 4096], P(None, None, 'cp')
- w_two: bfloat16 [3, 3, 4096, 1024], P(None, None, 'cp')
- bias_one: float32 [4096], replicated
Outputs:
- output: bfloat16 [32, 96, 14, 1024], P('dp', 'sp', None, 'cp')
All inputs are finite; a program needn't handle non-finite values.
Results may differ from a plain program's by a relative error of at most 0.001.
Values are sent between devices in bfloat16 or wider.
A program may use at most 1 GiB of HBM per device.

v0:
```python
import functools

import jax
import jax.numpy as jnp
from jax import lax
from jax.experimental import pallas as pl
from jax.experimental.pallas import tpu as pltpu
from jax.sharding import PartitionSpec as P

MESH = pl.DeviceIdType.MESH
N_STEPS = 64
MIB = 1024 * 1024
ONE, TWO, THREE, FOUR, ALL = (1,), (2,), (3,), (4,), (2, 16)
GRID, CUBE, HALVES = (2, 2), (2, 2, 2), (4, 2)
QUARTERS, ROWS = (4, 4), (4, 2, 4)
SEMS = (
    TWO, TWO, TWO, TWO, TWO, ONE, (2, 3), THREE, THREE, TWO, FOUR,
    HALVES, HALVES, QUARTERS, QUARTERS, QUARTERS, QUARTERS, ROWS, ROWS,
    CUBE, CUBE, GRID, GRID, GRID, GRID, CUBE, CUBE,
    ALL, ALL, TWO, TWO, ONE, ONE, ONE,
)


def pair(e):
    return e >> 1, e & 1


def each(first, stop, act):
    lax.fori_loop(first, stop, lambda e, carry: (act(e), carry)[1], 0)


def odd(i):
    return (i & 1) == 1


def swap_matrix(n):
    shift = n.bit_length() - 1
    to = lax.broadcasted_iota(jnp.int32, (n * n, n * n), 0)
    frm = lax.broadcasted_iota(jnp.int32, (n * n, n * n), 1)
    hit = ((to >> shift) == (frm & (n - 1))) & ((to & (n - 1)) == (frm >> shift))
    return jnp.where(hit, 1.0, 0.0).astype(jnp.bfloat16)


def fused_block(xw, w_one, w_two, bias):
    images, cols, h_loc, cb = xw.shape
    ni = images // 2
    rows = h_loc // 2
    m_rows = rows * ni
    tile = 2 * cb
    assert ni == 16 and h_loc == 48

    def remote(src, dst, send_sem, recv_sem, sp, cp):
        return pltpu.make_async_remote_copy(src_ref=src, dst_ref=dst, send_sem=send_sem, recv_sem=recv_sem,
                                            device_id={"sp": sp, "cp": cp}, device_id_type=MESH)

    def kernel(xw, w1, w2, b1, yt, g1, g2, part, hid,
               xa, acc, wv, stage, raw, swap, mark,
               wsem, asem, pst, pld, stl, zsem, rsem, xs, xr, hs, hr,
               p1s, p1r, x1s, x1r, y1s, y1r, f1s, f1r,
               p2s, p2r, x2s, x2r, y2s, y2r, f2s, f2r,
               as_, ar, ys, yr, zs, zr, yl):
        sp = lax.axis_index("sp")
        k = lax.axis_index("cp")
        x = (k >> 1)
        c = (k & 1)
        blk = 2 * sp + c
        osp = 1 - sp
        k1 = 2 * x + (1 - c)
        k2 = 2 * (1 - x) + c
        k3 = 2 * (1 - x) + (1 - c)

        def rarely(cond):
            def wrap(body):
                @pl.when(cond)
                def _():
                    mark[...] = jnp.zeros(mark.shape, jnp.float32)
                    body()

            return wrap

        def tile_of(xx, j, par):
            return 4 * ((xx + (j >> 1)) & 1) + 2 * (j & 1) + par

        barrier = pltpu.get_barrier_semaphore()
        for d_sp in range(2):
            for d_cp in range(4):
                if d_sp or d_cp:
                    pl.semaphore_signal(barrier, inc=1, device_id={"sp": ((sp + d_sp) & 1), "cp": ((k + d_cp) & 3)},
                                        device_id_type=MESH)

        def raw_load(far, part):
            cut = pl.ds(pl.multiple_of(ni * part, ni), ni)
            group = pl.ds(ni * (1 - x if far else x), ni)
            return pltpu.make_async_copy(xw.at[group, :, cut], raw.at[far, :, :, cut], rsem.at[far, part])

        def block(far, col, part):
            rows_in = raw[far, :, col, pl.ds(pl.multiple_of(ni * part, ni), ni), :].reshape(ni * ni, cb)
            out = jnp.dot(swap[...], rows_in, preferred_element_type=jnp.float32)
            return out.astype(jnp.bfloat16).reshape(ni, ni, cb)

        def slot_of(far, cc):
            return jnp.where(cc == c, 5 if far else 0, 6 if far else 4)

        def swap_end(far, cc):
            for col in range(cols):
                xa[slot_of(far, cc), pl.ds(1 + 8 * cc, ni), col] = block(far, col, 2 * cc)

        def swap_mid(far):
            for col in range(cols):
                mid = block(far, col, 1)
                xa[slot_of(far, 0), 17:26, col] = mid[0:9]
                xa[slot_of(far, 1), 0:9, col] = mid[7:16]

        def x_copy(role):
            cc = c if role == 2 else 1 - c
            cut = pl.ds(1 - cc, rows + 1)
            return remote(xa.at[3 + role, cut], xa.at[role, cut], xs.at[role - 1], xr.at[role - 1], sp,
                          {1: k1, 2: k2, 3: k3}[role])

        def halo_copy(far):
            xx = 1 - x if far else x
            role = 2 * ((x + xx) & 1) + ((c + sp) & 1)
            src = xa.at[slot_of(far, osp), jnp.where(sp == 0, rows, 1)]
            return remote(src, xa.at[role, (rows + 1) * sp], hs.at[far], hr.at[role], osp, 2 * xx + sp)

        piece = cb // 4

        def w1_own(j, par, xx):
            return w1.at[:, :, :, pl.ds(pl.multiple_of(tile_of(xx, j, par) * tile, tile), tile)]

        def w1_part(j, par):
            return remote(w1_own(j, par, x), g1.at[0, j, par], p1s.at[j, par], p1r.at[j, par], sp, k1)

        def w1_x(j, hf):
            cut = pl.ds(pl.multiple_of(hf * piece, piece), piece)
            src = w1.at[:, :, cut, pl.ds(pl.multiple_of(tile_of(1 - x, j, sp) * tile, tile), tile)]
            return remote(src, g1.at[1, j, sp, :, :, cut], x1s.at[j, hf], x1r.at[j, hf], sp, k2)

        def w1_y(j, hf):
            cut = pl.ds(pl.multiple_of(hf * piece, piece), piece)
            ref = g1.at[1, j, sp, :, :, cut]
            return remote(ref, ref, y1s.at[j, hf], y1r.at[j, hf], osp, k)

        def w1_fwd(j, par, hf):
            cut = pl.ds(pl.multiple_of(hf * piece, piece), piece)
            return remote(g1.at[1, j, par, :, :, cut], g1.at[2, j, par, :, :, cut], f1s.at[j, par, hf], f1r.at[j, par, hf], sp, k1)

        def w2_cut(n, par, h, xx):
            row = pl.multiple_of(par * tile + h * cb, cb)
            col = pl.multiple_of(tile * ((1 + xx + n) & 1), tile)
            return w2.at[:, :, pl.ds(row, cb), pl.ds(col, tile)]

        def w2_part(n, par, h):
            return remote(w2_cut(n, par, h, x), g2.at[0, n, par, h], p2s.at[n, par, h], p2r.at[n, par, h], sp, k1)

        def w2_x(n, h):
            return remote(w2_cut(n, sp, h, 1 - x), g2.at[1, n, sp, h], x2s.at[n, h], x2r.at[n, h], sp, k2)

        def w2_y(n, h):
            ref = g2.at[1, n, sp, h]
            return remote(ref, ref, y2s.at[n, h], y2r.at[n, h], osp, k)

        def w2_fwd(n, par, h):
            return remote(g2.at[1, n, par, h], g2.at[2, n, par, h], f2s.at[n, par, h], f2r.at[n, par, h], sp, k1)

        up_blk = lax.max(blk - 1, 0)
        dn_blk = lax.min(blk + 1, 3)

        def hid_up(a):
            return remote(hid.at[a, 1], hid.at[a, rows + 1], as_.at[0, a], ar.at[1, a], (up_blk >> 1), 2 * x + (up_blk & 1))

        def hid_dn(a):
            return remote(hid.at[a, rows], hid.at[a, 0], as_.at[1, a], ar.at[0, a], (dn_blk >> 1), 2 * x + (dn_blk & 1))

        def hid_store(a, h):
            return pltpu.make_async_copy(stage.at[h], hid.at[a, pl.ds(1, rows)], stl.at[h])

        y_rows = pl.ds(rows * c, rows)

        def y_far(h):
            return remote(stage.at[h], yt.at[x, y_rows], ys.at[h], yr.at[((h + c) & 1)], sp, 2 * (1 - x) + h)

        def y_near():
            return remote(stage.at[1 - c], yt.at[x, y_rows], zs.at[0], zr.at[0], sp, k1)

        def y_own():
            return pltpu.make_async_copy(stage.at[c], yt.at[x, y_rows], yl.at[0])

        def zero_rows(row):
            return pltpu.make_async_copy(stage.at[0, pl.ds(0, 16)], hid.at[:, row], zsem.at[0])

        def p_of(m):
            return (m + 2) & 7

        def jp(p):
            return p >> 1, (sp + p) & 1

        def send_w1_x(e):
            w1_x(e >> 2, e & 3).start()

        def near_step(i):
            return 2 * (i >> 2) + (i & 1), (i & 2) >> 1

        def halo_wait(role):
            @pl.when(c != sp)
            def _():
                remote(xa.at[0, 0], xa.at[role, 0], hs.at[0], hr.at[role], osp, k).wait_recv()

        for part_no in (2 * osp, 2 * sp, 1):
            raw_load(0, part_no).start()
        swap[...] = swap_matrix(ni)
        edge = c == sp

        @pl.when(edge)
        def _():
            xa[0:4, (rows + 1) * sp] = jnp.zeros((4, cols, ni, cb), jnp.bfloat16)

        def w_load(src, t):
            return pltpu.make_async_copy(src, wv.at[(t & 1)], wsem.at[(t & 1)])

        def hid_load(a, q):
            slot = (q & 1)
            return pltpu.make_async_copy(hid.at[a], xa.at[4 + slot], asem.at[slot])

        def issue(t):
            @rarely(t < 16)
            def _():
                m, role = near_step(t)
                j, par = jp(p_of(m))

                @rarely(role == 0)
                def _():
                    w_load(w1_own(j, par, x), t).start()

                @rarely(role == 1)
                def _():
                    w1_part(j, par).wait_recv()
                    w_load(g1.at[0, j, par], t).start()

            @rarely((t >= 16) & (t < 32))
            def _():
                j, par = jp(((t - 16) >> 1))

                @rarely((t & 1) == 1)
                def _():
                    for hf in range(4):
                        w1_fwd(j, par, hf).wait_recv()

                w_load(g1.at[1 + (t & 1), j, par], t).start()

            @rarely((t >= 32) & (t < N_STEPS))
            def _():
                n = ((t - 32) >> 4)
                q = ((t - 32) & 15)
                h = (q & 1)
                p = (q >> 1)
                j, par = jp(p)
                a = 4 * j + 2 * par + h
                same = (j & 1) == c

                @rarely(n == 0)
                def _():
                    @pl.when(blk > 0)
                    def _():
                        hid_dn(a).wait_recv()

                    @pl.when(blk < 3)
                    def _():
                        hid_up(a).wait_recv()

                hid_load(a, q).start()

                @rarely(p < 4)
                def _():
                    @rarely(same)
                    def _():
                        w_load(w2_cut(n, par, h, x), t).start()

                    @rarely(jnp.logical_not(same))
                    def _():
                        w2_part(n, par, h).wait_recv()
                        w_load(g2.at[0, n, par, h], t).start()

                @rarely(p >= 4)
                def _():
                    @pl.when(jnp.logical_not(same))
                    def _():
                        w2_fwd(n, par, h).wait_recv()

                    w_load(g2.at[jnp.where(same, 1, 2), n, par, h], t).start()

        raw_load(0, 2 * osp).wait()
        issue(jnp.int32(0))
        for part_no in range(3):
            raw_load(1, part_no).start()
        swap_end(0, osp)
        pl.semaphore_wait(barrier, 7)

        @pl.when(edge)
        def _():
            halo_copy(0).start()

        each(0, 6, send_w1_x)
        raw_load(0, 2 * sp).wait()
        raw_load(0, 1).wait()
        swap_end(0, sp)
        swap_mid(0)
        x_copy(1).start()
        for m in range(2):
            w1_part(*jp(jnp.int32(m + 2))).start()
        for part_no in range(3):
            raw_load(1, part_no).wait()
        for cc in range(2):
            swap_end(1, cc)
        swap_mid(1)
        halo_wait(0)

        def pass_w1_x(e):
            j, hf = e >> 2, e & 3
            w1_x(j, hf).wait_recv()
            w1_y(j, hf).start()
            w1_fwd(j, sp, hf).start()

        def pass_w1_y(e):
            j, hf = e >> 2, e & 3
            w1_y(j, hf).wait_recv()
            w1_fwd(j, osp, hf).start()

        def pass_w2_x(e):
            n, h = pair(e)
            w2_x(n, h).wait_recv()
            w2_y(n, h).start()
            w2_fwd(n, sp, h).start()

        def pass_w2_y(e):
            n, h = pair(e)
            w2_y(n, h).wait_recv()
            w2_fwd(n, osp, h).start()

        def send_w2_x(e):
            w2_x(*pair(e)).start()

        def events(i):
            is_odd = odd(i)
            even = jnp.logical_not(is_odd)

            @rarely(i < 16)
            def _():
                @rarely(even)
                def _():
                    @rarely(i < 12)
                    def _():
                        w1_part(*jp(p_of((i >> 1) + 2))).start()

                    @rarely(i == 2)
                    def _():
                        x_copy(1).wait_recv()
                        halo_wait(1)

                    @rarely(i == 10)
                    def _():
                        each(0, 4, pass_w1_y)

                    @rarely(i == 12)
                    def _():
                        each(4, 6, pass_w1_y)

                @rarely(is_odd)
                def _():
                    @rarely(i == 1)
                    def _():
                        @rarely(c != sp)
                        def _():
                            halo_copy(0).start()

                        halo_copy(1).start()

                        @rarely(edge)
                        def _():
                            stage[0, 0:16] = jnp.zeros((16, cols, ni, cb), jnp.bfloat16)
                            zero_rows((rows + 1) * sp).start()

                    @rarely(i == 3)
                    def _():
                        x_copy(2).start()

                    @rarely(i == 5)
                    def _():
                        each(0, 4, pass_w1_x)

                    @rarely(i == 7)
                    def _():
                        each(4, 6, pass_w1_x)

                    @rarely(i == 9)
                    def _():
                        x_copy(3).start()

            @rarely((i >= 13) & (i < 23))
            def _():
                send_w1_x(i - 7)

            @rarely((i >= 16) & (i < 34))
            def _():
                @rarely((i >= 18) & (i < 28))
                def _():
                    pass_w1_x(i - 12)

                @rarely((i >= 20) & (i < 30))
                def _():
                    pass_w1_y(i - 14)

                @rarely(i < 24)
                def _():
                    e = i - 16
                    w2_part((e >> 2), ((e >> 1) & 1), (e & 1)).start()

                @rarely(even)
                def _():
                    @rarely(i == 16)
                    def _():
                        x_copy(2).wait_recv()
                        halo_wait(2)

                    @rarely(i == 30)
                    def _():
                        x_copy(1).wait_send()
                        x_copy(2).wait_send()
                        x_copy(3).wait_send()
                        for far in range(2):
                            halo_copy(far).wait_send()

                    @rarely((i >= 24) & ((i & 3) == 0))
                    def _():
                        send_w2_x(((i - 24) >> 2))

                @rarely(is_odd)
                def _():
                    @rarely(i == 17)
                    def _():
                        x_copy(3).wait_recv()
                        halo_wait(3)

                    @rarely(i >= 19)
                    def _():
                        for h in range(2):
                            hid_store(0, h).wait()

                    @rarely(i >= 27)
                    def _():
                        for d in range(2):
                            j, par = jp(i - 27 + d)
                            for h in range(2):
                                a = 4 * j + 2 * par + h

                                @pl.when(blk > 0)
                                def _():
                                    hid_up(a).start()

                                @pl.when(blk < 3)
                                def _():
                                    hid_dn(a).start()

                    @rarely(i == 31)
                    def _():
                        pass_w2_x(jnp.int32(0))

            @rarely((i >= 34) & (i < 50))
            def _():
                @rarely(i == 36)
                def _():
                    send_w2_x(jnp.int32(3))

                @rarely((i < 44) & ((i & 3) == 3))
                def _():
                    pass_w2_x(((i - 31) >> 2))

                @rarely((i >= 37) & ((i & 3) == 1))
                def _():
                    pass_w2_y(((i - 37) >> 2))

        def taps(xs_slot, ws_slot, col, lanes=slice(None)):
            total = None
            for dx in (-1, 0, 1):
                if not 0 <= col + dx < cols:
                    continue
                for dy in range(3):
                    lhs = xa[xs_slot, dy:dy + rows, col + dx].reshape(m_rows, cb)
                    prod = jnp.dot(lhs, wv[ws_slot, dy, dx + 1, :, lanes], preferred_element_type=jnp.float32)
                    total = prod if total is None else total + prod
            return total

        def step(i, carry):
            ph1 = i < 16
            ph3 = i >= 32
            n = jnp.where(ph3, ((i - 32) >> 4), 0)
            q = jnp.where(ph3, ((i - 32) & 15), 0)
            m, role = near_step(i)
            m = jnp.where(ph1, m, ((i - 16) >> 1))
            role = jnp.where(ph1, role, 2 + (i & 1))
            p = jnp.where(ph1, p_of(m), (m & 7))
            p = jnp.where(ph3, 0, p)
            last = jnp.where(ph3, q == 15, role == 3)
            first = jnp.where(ph3, q == 0, role == 0)
            a_slot = jnp.where(ph3, n, (p & 1))
            x_slot = jnp.where(ph3, 4 + (q & 1), role)
            w_slot = (i & 1)

            events(i)
            issue(i + 1)
            w_load(g1.at[0, 0, 0], i).wait()

            @pl.when(ph3)
            def _():
                hid_load(0, q).wait()

            @rarely((i >= 4) & (i < 32))
            def _():
                @pl.when(ph1 & first)
                def _():
                    pltpu.make_async_copy(acc.at[a_slot], part.at[0], pst.at[a_slot]).wait()

                @pl.when((i >= 20) & (role == 2))
                def _():
                    pltpu.make_async_copy(part.at[0], acc.at[a_slot], pld.at[a_slot]).wait()

            @pl.when(jnp.logical_not(last))
            def _():
                for col in range(cols):
                    total = taps(x_slot, w_slot, col)
                    acc[a_slot, col] = total + jnp.where(first, 0.0, acc[a_slot, col])

            @rarely((i < 12) & (role == 1))
            def _():
                pltpu.make_async_copy(acc.at[a_slot], part.at[p], pst.at[a_slot]).start()

            @pl.when(last & (i < N_STEPS - 1))
            def _():
                @pl.when((i == 17) & edge)
                def _():
                    zero_rows(0).wait()

                keep = jnp.where(ph3, 1.0, 0.0)
                floor = jnp.where(ph3, -jnp.inf, 0.0)
                j, par = jp(p)
                shift = b1[tile_of(x, j, par)] * (1.0 - keep)
                for col in range(cols):
                    total = taps(x_slot, w_slot, col) + acc[a_slot, col] + shift
                    for h in range(2):
                        role = 2 + ((c + h) & 1)
                        res = xa[role, 1:rows + 1, col].reshape(m_rows, cb).astype(jnp.float32)
                        val = jnp.maximum(total[:, h * cb:(h + 1) * cb] + res * keep, floor)
                        stage[h, :, col] = val.astype(jnp.bfloat16).reshape(rows, ni, cb)

                @pl.when(i < 32)
                def _():
                    for h in range(2):
                        hid_store(4 * j + 2 * par + h, h).start()

                    @pl.when(p < 6)
                    def _():
                        pltpu.make_async_copy(part.at[p + 2], acc.at[a_slot], pld.at[a_slot]).start()

                @pl.when(i == 47)
                def _():
                    for h in range(2):
                        y_far(h).start()

            @pl.when(i == N_STEPS - 1)
            def _():
                for h in range(2):
                    y_far(h).wait_send()

                def half_step(own, carry):
                    h = jnp.where(own == 1, c, 1 - c)
                    lanes = pl.ds(pl.multiple_of(h * cb, cb), cb)
                    for col in range(cols):
                        total = taps(x_slot, w_slot, col, lanes) + acc[a_slot, col, :, lanes]
                        res = xa[1 - own, 1:rows + 1, col].reshape(m_rows, cb).astype(jnp.float32)
                        stage[h, :, col] = (total + res).astype(jnp.bfloat16).reshape(rows, ni, cb)

                    @pl.when(own == 0)
                    def _():
                        y_near().start()

                    return carry

                lax.fori_loop(0, 2, half_step, 0)
                y_own().start()

            return carry

        lax.fori_loop(0, N_STEPS, step, 0)

        def drain(e, carry):
            hi, lo = pair(e)
            w1_part(hi, lo).wait_send()
            for hf in (lo, lo + 2):
                w1_x(hi, hf).wait_send()
                w1_y(hi, hf).wait_send()
            for hf in range(4):
                w1_fwd(hi, lo, hf).wait_send()
            n, par = e >> 2, (e >> 1) & 1
            w2_part(n, par, lo).wait_send()
            w2_fwd(n, par, lo).wait_send()
            return carry

        lax.fori_loop(0, 8, drain, 0)

        def drain_rows(a, carry):
            @pl.when(blk > 0)
            def _():
                hid_up(a).wait_send()

            @pl.when(blk < 3)
            def _():
                hid_dn(a).wait_send()

            return carry

        lax.fori_loop(0, 16, drain_rows, 0)

        def drain_two(e, carry):
            w2_x(*pair(e)).wait_send()
            w2_y(*pair(e)).wait_send()
            return carry

        lax.fori_loop(0, 4, drain_two, 0)
        for e in range(2):
            remote(stage.at[0], yt.at[0, pl.ds(0, rows)], ys.at[0], yr.at[e], sp, k).wait_recv()
        y_near().wait()
        y_own().wait()

    dma = pltpu.SemaphoreType.DMA
    bf16, f32 = jnp.bfloat16, jnp.float32
    any_space = pl.BlockSpec(memory_space=pl.ANY)
    outs = pl.pallas_call(
        kernel,
        out_shape=[
            jax.ShapeDtypeStruct((2, h_loc, cols, ni, cb), bf16),
            jax.ShapeDtypeStruct((3, 4, 2, 3, 3, cb, tile), bf16),
            jax.ShapeDtypeStruct((3, 2, 2, 2, 3, 3, cb, tile), bf16),
            jax.ShapeDtypeStruct((8, cols, m_rows, tile), f32),
            jax.ShapeDtypeStruct((16, rows + 2, cols, ni, cb), bf16),
        ],
        in_specs=[any_space, any_space, any_space, pl.BlockSpec(memory_space=pltpu.VMEM)],
        out_specs=[any_space] * 5,
        scratch_shapes=[
            pltpu.VMEM((7, rows + 2, cols, ni, cb), bf16),
            pltpu.VMEM((2, cols, m_rows, tile), f32),
            pltpu.VMEM((2, 3, 3, cb, tile), bf16),
            pltpu.VMEM((2, rows, cols, ni, cb), bf16),
            pltpu.VMEM((2, ni, cols, h_loc, cb), bf16),
            pltpu.VMEM((ni * ni, ni * ni), bf16),
            pltpu.VMEM((8, 128), f32),
            *map(dma, SEMS),
        ],
        compiler_params=pltpu.CompilerParams(collective_id=0, has_side_effects=True, vmem_limit_bytes=63 * MIB),
        name="fused_block",
    )(xw, w_one, w_two, bias)
    return outs[0]


def images_major(yt):
    groups, h_loc, cols, ni, cb = yt.shape
    parts = h_loc // ni
    width = cols // 2
    chunks = groups * parts * 2
    assert ni == 16

    def kernel(y, out, y_in, y_out, swap, in_sem, out_sem):
        def place(e):
            block, side = pair(e)
            group, part = lax.div(block, parts), lax.rem(block, parts)
            n0, h0 = pl.multiple_of(ni * group, ni), pl.multiple_of(ni * part, ni)
            return group, n0, h0, width * side

        def load(e):
            group, _, h0, col = place(e)
            cut = (group, pl.ds(h0, ni), pl.ds(col, width))
            return pltpu.make_async_copy(y.at[cut], y_in.at[cut], in_sem.at[e])

        def store(e):
            _, n0, h0, col = place(e)
            cut = (pl.ds(n0, ni), pl.ds(col, width), pl.ds(h0, ni))
            return pltpu.make_async_copy(y_out.at[cut], out.at[cut], out_sem.at[e])

        for e in range(chunks):
            load(jnp.int32(e)).start()
        swap[...] = swap_matrix(ni)

        def chunk(e, carry):
            load(e).wait()
            group, n0, h0, base = place(e)
            for col in range(width):
                rows_in = y_in[group, pl.ds(h0, ni), base + col].reshape(ni * ni, cb)
                res = jnp.dot(swap[...], rows_in, preferred_element_type=jnp.float32)
                y_out[pl.ds(n0, ni), base + col, pl.ds(h0, ni)] = res.astype(jnp.bfloat16).reshape(ni, ni, cb)
            store(e).start()
            return carry

        lax.fori_loop(0, chunks, chunk, 0)
        for e in range(chunks):
            store(jnp.int32(e)).wait()

    dma = pltpu.SemaphoreType.DMA
    out_shape = (groups * ni, cols, h_loc, cb)
    return pl.pallas_call(
        kernel,
        out_shape=jax.ShapeDtypeStruct(out_shape, jnp.bfloat16),
        in_specs=[pl.BlockSpec(memory_space=pl.ANY)],
        out_specs=pl.BlockSpec(memory_space=pl.ANY),
        scratch_shapes=[pltpu.VMEM(yt.shape, jnp.bfloat16), pltpu.VMEM(out_shape, jnp.bfloat16), pltpu.VMEM((ni * ni, ni * ni), jnp.bfloat16),
                        dma((chunks,)), dma((chunks,))],
        compiler_params=pltpu.CompilerParams(vmem_limit_bytes=63 * MIB),
        name="images_major",
    )(yt)


def solution(mesh):
    act_spec = P("dp", "sp", None, "cp")
    kernel_spec = P(None, None, "cp", None)

    def local_block(x_tile, w_one_part, w_two_part, bias_one):
        xw = x_tile.transpose(0, 2, 1, 3)
        yt = fused_block(xw, w_one_part, w_two_part, bias_one.reshape(8, 1, 2 * x_tile.shape[3]))
        return images_major(yt).transpose(0, 2, 1, 3)

    return jax.shard_map(local_block, mesh=mesh, in_specs=(act_spec, kernel_spec, kernel_spec, P()), out_specs=act_spec, check_vma=False)
```

profile of v0, /device:TPU:0, one launch (start us, length us, event | category | flops | bytes accessed | tf_op | source)
XLA Modules:
  0.0 820.5 jit_solution(2214437283788107919)
XLA Ops:
  0.0 811.9 %fused_block.1 = (bf16[2,48,14,16,256]{4,3,2,1,0:T(8,128)(2,1)}, bf16[3,4,2,3,3,256,512]{6,5,4,3,2,1,0:T(8,128)(2,1)}, bf16[3,2,2,2,3,3,256,512]{7,6,5,4,3,2,1,0...) custom-call(bf16[32,14,48,256]{3,2,1,0:T(8,128)(2,1)} %bitcast.3, bf16[3,3,256,4096]{3,2,1,0:T(8,128)(2,1)} %w1.1, ...), custom_call_target="tpu_custom_call" | custom-call | tf_op jit(solution)/shard_map/fused_block/pallas_call | solution.py:637
  811.9 8.4 %images_major.1 = bf16[32,14,48,256]{3,2,1,0:T(8,128)(2,1)} custom-call(bf16[2,48,14,16,256]{4,3,2,1,0:T(8,128)(2,1)} %get-tuple-element.6.y), custom_call_target="tpu_custom_call" | custom-call | tf_op jit(solution)/shard_map/images_major/pallas_call | solution.py:708
where the time goes:
time: 821 us; the launch traced here: 820 us
  Pallas kernels  820 us (100%)
    pallas_call x1, Pallas kernels, fused_block(): pl.pallas_call(kernel, out_shape=[jax.ShapeDtypeStruct((2, h_loc, cols, n...  812 us

commit v1 on v0

--- a/solution.py
+++ b/solution.py
@@ -270,24 +270,23 @@
 
                 hid_load(a, q).start()
 
-                @rarely(p < 4)
-                def _():
-                    @rarely(same)
-                    def _():
-                        w_load(w2_cut(n, par, h, x), t).start()
-
-                    @rarely(jnp.logical_not(same))
+                own = (p < 4) & same
+
+                @rarely(own)
+                def _():
+                    w_load(w2_cut(n, par, h, x), t).start()
+
+                @rarely(jnp.logical_not(own))
+                def _():
+                    @pl.when(p < 4)
                     def _():
                         w2_part(n, par, h).wait_recv()
-                        w_load(g2.at[0, n, par, h], t).start()
-
-                @rarely(p >= 4)
-                def _():
-                    @pl.when(jnp.logical_not(same))
+
+                    @pl.when((p >= 4) & jnp.logical_not(same))
                     def _():
                         w2_fwd(n, par, h).wait_recv()
 
-                    w_load(g2.at[jnp.where(same, 1, 2), n, par, h], t).start()
+                    w_load(g2.at[jnp.where(p < 4, 0, jnp.where(same, 1, 2)), n, par, h], t).start()
 
         raw_load(0, 2 * osp).wait()
         issue(jnp.int32(0))
@@ -341,6 +340,11 @@
             w2_x(*pair(e)).start()
 
         def events(i):
+            @rarely(i < 50)
+            def _():
+                early_events(i)
+
+        def early_events(i):
             is_odd = odd(i)
             even = jnp.logical_not(is_odd)
 
@@ -465,7 +469,7 @@
                     def _():
                         pass_w2_x(jnp.int32(0))
 
-            @rarely((i >= 34) & (i < 50))
+            @rarely(i >= 34)
             def _():
                 @rarely(i == 36)
                 def _():
@@ -530,63 +534,62 @@
                     total = taps(x_slot, w_slot, col)
                     acc[a_slot, col] = total + jnp.where(first, 0.0, acc[a_slot, col])
 
-            @rarely((i < 12) & (role == 1))
-            def _():
-                pltpu.make_async_copy(acc.at[a_slot], part.at[p], pst.at[a_slot]).start()
-
-            @pl.when(last & (i < N_STEPS - 1))
-            def _():
+                @rarely((i < 12) & (role == 1))
+                def _():
+                    pltpu.make_async_copy(acc.at[a_slot], part.at[p], pst.at[a_slot]).start()
+
+            def finish_hidden():
                 @pl.when((i == 17) & edge)
                 def _():
                     zero_rows(0).wait()
 
-                keep = jnp.where(ph3, 1.0, 0.0)
-                floor = jnp.where(ph3, -jnp.inf, 0.0)
                 j, par = jp(p)
-                shift = b1[tile_of(x, j, par)] * (1.0 - keep)
+                shift = b1[tile_of(x, j, par)]
                 for col in range(cols):
-                    total = taps(x_slot, w_slot, col) + acc[a_slot, col] + shift
+                    val = jnp.maximum(taps(x_slot, w_slot, col) + acc[a_slot, col] + shift, 0.0).astype(jnp.bfloat16)
                     for h in range(2):
-                        role = 2 + ((c + h) & 1)
-                        res = xa[role, 1:rows + 1, col].reshape(m_rows, cb).astype(jnp.float32)
-                        val = jnp.maximum(total[:, h * cb:(h + 1) * cb] + res * keep, floor)
-                        stage[h, :, col] = val.astype(jnp.bfloat16).reshape(rows, ni, cb)
-
-                @pl.when(i < 32)
+                        stage[h, :, col] = val[:, h * cb:(h + 1) * cb].reshape(rows, ni, cb)
+                for h in range(2):
+                    hid_store(4 * j + 2 * par + h, h).start()
+
+                @pl.when(p < 6)
+                def _():
+                    pltpu.make_async_copy(part.at[p + 2], acc.at[a_slot], pld.at[a_slot]).start()
+
+            def finish_out():
+                @pl.when(n == 1)
                 def _():
                     for h in range(2):
-                        hid_store(4 * j + 2 * par + h, h).start()
-
-                    @pl.when(p < 6)
-                    def _():
-                        pltpu.make_async_copy(part.at[p + 2], acc.at[a_slot], pld.at[a_slot]).start()
-
-                @pl.when(i == 47)
-                def _():
-                    for h in range(2):
-                        y_far(h).start()
-
-            @pl.when(i == N_STEPS - 1)
-            def _():
-                for h in range(2):
-                    y_far(h).wait_send()
-
-                def half_step(own, carry):
-                    h = jnp.where(own == 1, c, 1 - c)
+                        y_far(h).wait_send()
+
+                def half_step(same, carry):
+                    h = jnp.where(same == 1, c, 1 - c)
                     lanes = pl.ds(pl.multiple_of(h * cb, cb), cb)
                     for col in range(cols):
                         total = taps(x_slot, w_slot, col, lanes) + acc[a_slot, col, :, lanes]
-                        res = xa[1 - own, 1:rows + 1, col].reshape(m_rows, cb).astype(jnp.float32)
+                        res = xa[3 - 2 * n - same, 1:rows + 1, col].reshape(m_rows, cb).astype(jnp.float32)
                         stage[h, :, col] = (total + res).astype(jnp.bfloat16).reshape(rows, ni, cb)
 
-                    @pl.when(own == 0)
+                    @pl.when(n == 0)
+                    def _():
+                        y_far(h).start()
+
+                    @pl.when((n == 1) & (same == 0))
                     def _():
                         y_near().start()
 
                     return carry
 
                 lax.fori_loop(0, 2, half_step, 0)
-                y_own().start()
+
+                @pl.when(n == 1)
+                def _():
+                    y_own().start()
+
+            @pl.when(last)
+            def _():
+                pl.when(jnp.logical_not(ph3))(finish_hidden)
+                pl.when(ph3)(finish_out)
 
             return carry
 

time: 821 us -> 820 us (level)
  no operation moved by 1% of the time
where the time goes in v1:
time: 820 us; the launch traced here: 819 us
  Pallas kernels  819 us (100%)
    pallas_call x1, Pallas kernels, fused_block(): pl.pallas_call(kernel, out_shape=[jax.ShapeDtypeStruct((2, h_loc, cols, n...  811 us

profile of v1, /device:TPU:0, one launch (start us, length us, event | category | flops | bytes accessed | tf_op | source)
XLA Modules:
  0.0 819.4 jit_solution(1487755676066579118)
XLA Ops:
  0.0 810.8 %fused_block.1 = (bf16[2,48,14,16,256]{4,3,2,1,0:T(8,128)(2,1)}, bf16[3,4,2,3,3,256,512]{6,5,4,3,2,1,0:T(8,128)(2,1)}, bf16[3,2,2,2,3,3,256,512]{7,6,5,4,3,2,1,0...) custom-call(bf16[32,14,48,256]{3,2,1,0:T(8,128)(2,1)} %bitcast.3, bf16[3,3,256,4096]{3,2,1,0:T(8,128)(2,1)} %w1.1, ...), custom_call_target="tpu_custom_call" | custom-call | tf_op jit(solution)/shard_map/fused_block/pallas_call | solution.py:640
  810.8 8.4 %images_major.1 = bf16[32,14,48,256]{3,2,1,0:T(8,128)(2,1)} custom-call(bf16[2,48,14,16,256]{4,3,2,1,0:T(8,128)(2,1)} %get-tuple-element.6.y), custom_call_target="tpu_custom_call" | custom-call | tf_op jit(solution)/shard_map/images_major/pallas_call | solution.py:711

commit v2 on v1

--- a/solution.py
+++ b/solution.py
@@ -82,11 +82,8 @@
             return 4 * ((xx + (j >> 1)) & 1) + 2 * (j & 1) + par
 
         barrier = pltpu.get_barrier_semaphore()
-        for d_sp in range(2):
-            for d_cp in range(4):
-                if d_sp or d_cp:
-                    pl.semaphore_signal(barrier, inc=1, device_id={"sp": ((sp + d_sp) & 1), "cp": ((k + d_cp) & 3)},
-                                        device_id_type=MESH)
+        for to_sp, to_cp in ((sp, k1), (sp, k2), (sp, k3), (osp, k), (osp, k1)):
+            pl.semaphore_signal(barrier, inc=1, device_id={"sp": to_sp, "cp": to_cp}, device_id_type=MESH)
 
         def raw_load(far, part):
             cut = pl.ds(pl.multiple_of(ni * part, ni), ni)
@@ -293,7 +290,7 @@
         for part_no in range(3):
             raw_load(1, part_no).start()
         swap_end(0, osp)
-        pl.semaphore_wait(barrier, 7)
+        pl.semaphore_wait(barrier, 5)
 
         @pl.when(edge)
         def _():
@@ -377,8 +374,6 @@
                         def _():
                             halo_copy(0).start()
 
-                        halo_copy(1).start()
-
                         @rarely(edge)
                         def _():
                             stage[0, 0:16] = jnp.zeros((16, cols, ni, cb), jnp.bfloat16)
@@ -395,6 +390,7 @@
                     @rarely(i == 7)
                     def _():
                         each(4, 6, pass_w1_x)
+                        halo_copy(1).start()
 
                     @rarely(i == 9)
                     def _():

time: 820 us -> 820 us (level)
  no operation moved by 1% of the time
where the time goes in v2:
time: 820 us; the launch traced here: 819 us
  Pallas kernels  819 us (100%)
    pallas_call x1, Pallas kernels, fused_block(): pl.pallas_call(kernel, out_shape=[jax.ShapeDtypeStruct((2, h_loc, cols, n...  811 us

profile of v2, /device:TPU:0, one launch (start us, length us, event | category | flops | bytes accessed | tf_op | source)
XLA Modules:
  0.0 819.5 jit_solution(8755309525776275084)
XLA Ops:
  0.0 810.9 %fused_block.1 = (bf16[2,48,14,16,256]{4,3,2,1,0:T(8,128)(2,1)}, bf16[3,4,2,3,3,256,512]{6,5,4,3,2,1,0:T(8,128)(2,1)}, bf16[3,2,2,2,3,3,256,512]{7,6,5,4,3,2,1,0...) custom-call(bf16[32,14,48,256]{3,2,1,0:T(8,128)(2,1)} %bitcast.3, bf16[3,3,256,4096]{3,2,1,0:T(8,128)(2,1)} %w1.1, ...), custom_call_target="tpu_custom_call" | custom-call | tf_op jit(solution)/shard_map/fused_block/pallas_call | solution.py:636
  810.9 8.4 %images_major.1 = bf16[32,14,48,256]{3,2,1,0:T(8,128)(2,1)} custom-call(bf16[2,48,14,16,256]{4,3,2,1,0:T(8,128)(2,1)} %get-tuple-element.6.y), custom_call_target="tpu_custom_call" | custom-call | tf_op jit(solution)/shard_map/images_major/pallas_call | solution.py:707

commit v3 on v2

--- a/solution.py
+++ b/solution.py
@@ -54,7 +54,7 @@
                                             device_id={"sp": sp, "cp": cp}, device_id_type=MESH)
 
     def kernel(xw, w1, w2, b1, yt, g1, g2, part, hid,
-               xa, acc, wv, stage, raw, swap, mark,
+               xa, acc, wv, stage, raw, swap, mark, shifts, bsem,
                wsem, asem, pst, pld, stl, zsem, rsem, xs, xr, hs, hr,
                p1s, p1r, x1s, x1r, y1s, y1r, f1s, f1r,
                p2s, p2r, x2s, x2r, y2s, y2r, f2s, f2r,
@@ -120,6 +120,9 @@
             src = xa.at[slot_of(far, osp), jnp.where(sp == 0, rows, 1)]
             return remote(src, xa.at[role, (rows + 1) * sp], hs.at[far], hr.at[role], osp, 2 * xx + sp)
 
+        def bias_load():
+            return pltpu.make_async_copy(b1, shifts, bsem.at[0])
+
         piece = cb // 4
 
         def w1_own(j, par, xx):
@@ -289,6 +292,7 @@
         issue(jnp.int32(0))
         for part_no in range(3):
             raw_load(1, part_no).start()
+        bias_load().start()
         swap_end(0, osp)
         pl.semaphore_wait(barrier, 5)
 
@@ -419,6 +423,7 @@
                 def _():
                     @rarely(i == 16)
                     def _():
+                        bias_load().wait()
                         x_copy(2).wait_recv()
                         halo_wait(2)
 
@@ -540,7 +545,7 @@
                     zero_rows(0).wait()
 
                 j, par = jp(p)
-                shift = b1[tile_of(x, j, par)]
+                shift = shifts[tile_of(x, j, par)]
                 for col in range(cols):
                     val = jnp.maximum(taps(x_slot, w_slot, col) + acc[a_slot, col] + shift, 0.0).astype(jnp.bfloat16)
                     for h in range(2):
@@ -642,7 +647,7 @@
             jax.ShapeDtypeStruct((8, cols, m_rows, tile), f32),
             jax.ShapeDtypeStruct((16, rows + 2, cols, ni, cb), bf16),
         ],
-        in_specs=[any_space, any_space, any_space, pl.BlockSpec(memory_space=pltpu.VMEM)],
+        in_specs=[any_space] * 4,
         out_specs=[any_space] * 5,
         scratch_shapes=[
             pltpu.VMEM((7, rows + 2, cols, ni, cb), bf16),
@@ -652,6 +657,8 @@
             pltpu.VMEM((2, ni, cols, h_loc, cb), bf16),
             pltpu.VMEM((ni * ni, ni * ni), bf16),
             pltpu.VMEM((8, 128), f32),
+            pltpu.VMEM(bias.shape, f32),
+            dma(ONE),
             *map(dma, SEMS),
         ],
         compiler_params=pltpu.CompilerParams(collective_id=0, has_side_effects=True, vmem_limit_bytes=63 * MIB),

time: 820 us -> 819 us (level)
  no operation moved by 1% of the time
where the time goes in v3:
time: 819 us
  Pallas kernels  819 us (100%)
    pallas_call x1, Pallas kernels, fused_block(): pl.pallas_call(kernel, out_shape=[jax.ShapeDtypeStruct((2, h_loc, cols, n...  810 us

profile of v3, /device:TPU:0, one launch (start us, length us, event | category | flops | bytes accessed | tf_op | source)
XLA Modules:
  0.0 818.8 jit_solution(721245235855556304)
XLA Ops:
  0.0 810.2 %fused_block.1 = (bf16[2,48,14,16,256]{4,3,2,1,0:T(8,128)(2,1)}, bf16[3,4,2,3,3,256,512]{6,5,4,3,2,1,0:T(8,128)(2,1)}, bf16[3,2,2,2,3,3,256,512]{7,6,5,4,3,2,1,0...) custom-call(bf16[32,14,48,256]{3,2,1,0:T(8,128)(2,1)} %bitcast.3, bf16[3,3,256,4096]{3,2,1,0:T(8,128)(2,1)} %w1.1, ...), custom_call_target="tpu_custom_call" | custom-call | tf_op jit(solution)/shard_map/fused_block/pallas_call | solution.py:641
  810.2 8.4 %images_major.1 = bf16[32,14,48,256]{3,2,1,0:T(8,128)(2,1)} custom-call(bf16[2,48,14,16,256]{4,3,2,1,0:T(8,128)(2,1)} %get-tuple-element.6.y), custom_call_target="tpu_custom_call" | custom-call | tf_op jit(solution)/shard_map/images_major/pallas_call | solution.py:714

commit v4 on v3

--- a/solution.py
+++ b/solution.py
@@ -15,9 +15,9 @@
 QUARTERS, ROWS = (4, 4), (4, 2, 4)
 SEMS = (
     TWO, TWO, TWO, TWO, TWO, ONE, (2, 3), THREE, THREE, TWO, FOUR,
-    HALVES, HALVES, QUARTERS, QUARTERS, QUARTERS, QUARTERS, ROWS, ROWS,
-    CUBE, CUBE, GRID, GRID, GRID, GRID, CUBE, CUBE,
-    ALL, ALL, TWO, TWO, ONE, ONE, ONE,
+    ONE, HALVES, ONE, QUARTERS, ONE, QUARTERS, ONE, ROWS,
+    ONE, CUBE, ONE, GRID, ONE, GRID, ONE, CUBE,
+    TWO, ALL, TWO, TWO, ONE, ONE, ONE,
 )
 
 
@@ -129,21 +129,21 @@
             return w1.at[:, :, :, pl.ds(pl.multiple_of(tile_of(xx, j, par) * tile, tile), tile)]
 
         def w1_part(j, par):
-            return remote(w1_own(j, par, x), g1.at[0, j, par], p1s.at[j, par], p1r.at[j, par], sp, k1)
+            return remote(w1_own(j, par, x), g1.at[0, j, par], p1s.at[0], p1r.at[j, par], sp, k1)
 
         def w1_x(j, hf):
             cut = pl.ds(pl.multiple_of(hf * piece, piece), piece)
             src = w1.at[:, :, cut, pl.ds(pl.multiple_of(tile_of(1 - x, j, sp) * tile, tile), tile)]
-            return remote(src, g1.at[1, j, sp, :, :, cut], x1s.at[j, hf], x1r.at[j, hf], sp, k2)
+            return remote(src, g1.at[1, j, sp, :, :, cut], x1s.at[0], x1r.at[j, hf], sp, k2)
 
         def w1_y(j, hf):
             cut = pl.ds(pl.multiple_of(hf * piece, piece), piece)
             ref = g1.at[1, j, sp, :, :, cut]
-            return remote(ref, ref, y1s.at[j, hf], y1r.at[j, hf], osp, k)
+            return remote(ref, ref, y1s.at[0], y1r.at[j, hf], osp, k)
 
         def w1_fwd(j, par, hf):
             cut = pl.ds(pl.multiple_of(hf * piece, piece), piece)
-            return remote(g1.at[1, j, par, :, :, cut], g1.at[2, j, par, :, :, cut], f1s.at[j, par, hf], f1r.at[j, par, hf], sp, k1)
+            return remote(g1.at[1, j, par, :, :, cut], g1.at[2, j, par, :, :, cut], f1s.at[0], f1r.at[j, par, hf], sp, k1)
 
         def w2_cut(n, par, h, xx):
             row = pl.multiple_of(par * tile + h * cb, cb)
@@ -151,26 +151,26 @@
             return w2.at[:, :, pl.ds(row, cb), pl.ds(col, tile)]
 
         def w2_part(n, par, h):
-            return remote(w2_cut(n, par, h, x), g2.at[0, n, par, h], p2s.at[n, par, h], p2r.at[n, par, h], sp, k1)
+            return remote(w2_cut(n, par, h, x), g2.at[0, n, par, h], p2s.at[0], p2r.at[n, par, h], sp, k1)
 
         def w2_x(n, h):
-            return remote(w2_cut(n, sp, h, 1 - x), g2.at[1, n, sp, h], x2s.at[n, h], x2r.at[n, h], sp, k2)
+            return remote(w2_cut(n, sp, h, 1 - x), g2.at[1, n, sp, h], x2s.at[0], x2r.at[n, h], sp, k2)
 
         def w2_y(n, h):
             ref = g2.at[1, n, sp, h]
-            return remote(ref, ref, y2s.at[n, h], y2r.at[n, h], osp, k)
+            return remote(ref, ref, y2s.at[0], y2r.at[n, h], osp, k)
 
         def w2_fwd(n, par, h):
-            return remote(g2.at[1, n, par, h], g2.at[2, n, par, h], f2s.at[n, par, h], f2r.at[n, par, h], sp, k1)
+            return remote(g2.at[1, n, par, h], g2.at[2, n, par, h], f2s.at[0], f2r.at[n, par, h], sp, k1)
 
         up_blk = lax.max(blk - 1, 0)
         dn_blk = lax.min(blk + 1, 3)
 
         def hid_up(a):
-            return remote(hid.at[a, 1], hid.at[a, rows + 1], as_.at[0, a], ar.at[1, a], (up_blk >> 1), 2 * x + (up_blk & 1))
+            return remote(hid.at[a, 1], hid.at[a, rows + 1], as_.at[0], ar.at[1, a], (up_blk >> 1), 2 * x + (up_blk & 1))
 
         def hid_dn(a):
-            return remote(hid.at[a, rows], hid.at[a, 0], as_.at[1, a], ar.at[0, a], (dn_blk >> 1), 2 * x + (dn_blk & 1))
+            return remote(hid.at[a, rows], hid.at[a, 0], as_.at[1], ar.at[0, a], (dn_blk >> 1), 2 * x + (dn_blk & 1))
 
         def hid_store(a, h):
             return pltpu.make_async_copy(stage.at[h], hid.at[a, pl.ds(1, rows)], stl.at[h])
@@ -596,40 +596,18 @@
 
         lax.fori_loop(0, N_STEPS, step, 0)
 
-        def drain(e, carry):
-            hi, lo = pair(e)
-            w1_part(hi, lo).wait_send()
-            for hf in (lo, lo + 2):
-                w1_x(hi, hf).wait_send()
-                w1_y(hi, hf).wait_send()
-            for hf in range(4):
-                w1_fwd(hi, lo, hf).wait_send()
-            n, par = e >> 2, (e >> 1) & 1
-            w2_part(n, par, lo).wait_send()
-            w2_fwd(n, par, lo).wait_send()
-            return carry
-
-        lax.fori_loop(0, 8, drain, 0)
-
-        def drain_rows(a, carry):
-            @pl.when(blk > 0)
-            def _():
-                hid_up(a).wait_send()
-
-            @pl.when(blk < 3)
-            def _():
-                hid_dn(a).wait_send()
-
-            return carry
-
-        lax.fori_loop(0, 16, drain_rows, 0)
-
-        def drain_two(e, carry):
-            w2_x(*pair(e)).wait_send()
-            w2_y(*pair(e)).wait_send()
-            return carry
-
-        lax.fori_loop(0, 4, drain_two, 0)
+        for ref, sem in ((g1.at[0], p1s), (g1.at[1, :, 0], x1s), (g1.at[1, :, 0], y1s), (g1.at[2], f1s),
+                         (g2.at[0], p2s), (g2.at[1, :, 0], x2s), (g2.at[1, :, 0], y2s), (g2.at[2], f2s)):
+            remote(ref, ref, sem.at[0], zr.at[0], sp, k1).wait_send()
+
+        @pl.when(blk > 0)
+        def _():
+            remote(hid.at[:, 0], hid.at[:, 0], as_.at[0], zr.at[0], sp, k1).wait_send()
+
+        @pl.when(blk < 3)
+        def _():
+            remote(hid.at[:, 0], hid.at[:, 0], as_.at[1], zr.at[0], sp, k1).wait_send()
+
         for e in range(2):
             remote(stage.at[0], yt.at[0, pl.ds(0, rows)], ys.at[0], yr.at[e], sp, k).wait_recv()
         y_near().wait()

time: 819 us -> 818 us (level)
  no operation moved by 1% of the time
where the time goes in v4:
time: 818 us
  Pallas kernels  818 us (100%)
    pallas_call x1, Pallas kernels, fused_block(): pl.pallas_call(kernel, out_shape=[jax.ShapeDtypeStruct((2, h_loc, cols, n...  809 us

profile of v4, /device:TPU:0, one launch (start us, length us, event | category | flops | bytes accessed | tf_op | source)
XLA Modules:
  0.0 817.7 jit_solution(7077995887089618425)
XLA Ops:
  0.0 809.1 %fused_block.1 = (bf16[2,48,14,16,256]{4,3,2,1,0:T(8,128)(2,1)}, bf16[3,4,2,3,3,256,512]{6,5,4,3,2,1,0:T(8,128)(2,1)}, bf16[3,2,2,2,3,3,256,512]{7,6,5,4,3,2,1,0...) custom-call(bf16[32,14,48,256]{3,2,1,0:T(8,128)(2,1)} %bitcast.3, bf16[3,3,256,4096]{3,2,1,0:T(8,128)(2,1)} %w1.1, ...), custom_call_target="tpu_custom_call" | custom-call | tf_op jit(solution)/shard_map/fused_block/pallas_call | solution.py:619
  809.1 8.4 %images_major.1 = bf16[32,14,48,256]{3,2,1,0:T(8,128)(2,1)} custom-call(bf16[2,48,14,16,256]{4,3,2,1,0:T(8,128)(2,1)} %get-tuple-element.6.y), custom_call_target="tpu_custom_call" | custom-call | tf_op jit(solution)/shard_map/images_major/pallas_call | solution.py:692
